TPU v7x, 256 devices: a whole 4x4x8 slice. The times are simulated.
256 devices in a mesh: rows: 32 (over z, y), tp: 4 (over x), unit: 2 (over core).
Axes of the slice: x: 4, y: 4, z: 8, core: 2. Of those that a mesh axis runs over, the one named last changes fastest.
Arguments:
- w_query: bfloat16 [5120, 4096], P(('unit', 'rows'), 'tp'), parts along dimension 0, may hold values from -0.125 to 0.125
- low_query: bfloat16 [5120, 64], P(('unit', 'rows')), parts along dimension 0, may hold values from -0.125 to 0.125
- high_query: bfloat16 [128, 4096], P('unit', 'tp'), parts along dimension 0, may hold values from -0.75 to 0.75
- w_key: bfloat16 [5120, 1024], P(('unit', 'rows'), 'tp'), parts along dimension 0, may hold values from -0.125 to 0.125
- low_key: bfloat16 [5120, 64], P(('unit', 'rows')), parts along dimension 0, may hold values from -0.125 to 0.125
- high_key: bfloat16 [128, 1024], P('unit', 'tp'), parts along dimension 0, may hold values from -0.75 to 0.75
- w_value: bfloat16 [5120, 1024], P(('unit', 'rows'), 'tp'), parts along dimension 0, may hold values from -0.125 to 0.125
- low_value: bfloat16 [5120, 64], P(('unit', 'rows')), parts along dimension 0, may hold values from -0.125 to 0.125
- high_value: bfloat16 [128, 1024], P('unit', 'tp'), parts along dimension 0, may hold values from -0.75 to 0.75
- w_mixed: bfloat16 [8192, 2560], P(('unit', 'tp'), 'rows'), parts along dimension 0, may hold values from -0.09375 to 0.09375
- low_mixed: bfloat16 [8192, 64], P(('unit', 'tp')), parts along dimension 0, may hold values from -0.09375 to 0.09375
- high_mixed: bfloat16 [128, 2560], P('unit', 'rows'), parts along dimension 0, may hold values from -0.75 to 0.75
- norm_train: float32 [5120], P(('unit', 'rows', 'tp')), parts along dimension 0, may hold values from 0.25 to 1.75
- norm_step: float32 [5120], P(('unit', 'rows', 'tp')), parts along dimension 0, may hold values from -0.3 to 0.3
Outputs:
- final_query: bfloat16 [5120, 4096], P('unit', 'tp'), parts along dimension 0
- final_key: bfloat16 [5120, 1024], P('unit', 'tp'), parts along dimension 0
- final_value: bfloat16 [5120, 1024], P('unit', 'tp'), parts along dimension 0
- final_mixed: bfloat16 [8192, 2560], P(('unit', 'tp')), parts along dimension 0
- serve_norm: bfloat16 [5120], P('unit'), parts along dimension 0
There are 2 independent parts, one for each index of `unit`. A program takes and returns all parts, laid end to end along the dimension named above; each array names one. Nothing has to cross between parts.
All inputs are finite; a program needn't handle non-finite values.
Results may differ from a plain program's by a relative error of at most 0.001.
Values may be sent and summed in bfloat16 or wider, within the bound.
A program may use at most 128 MiB of HBM per device.

v0:
```python
import jax
import jax.numpy as jnp
from jax import lax
from jax.sharding import Mesh
from jax.sharding import PartitionSpec as P

ROWS = ("rows_0", "rows_1")
ROWS_TP = ("rows_0", "rows_1", "tp")
UNIT_ROWS = ("unit", "rows_0", "rows_1")
UNIT_ROWS_TP = ("unit", "rows_0", "rows_1", "tp")


mix_rate = 0.5


def gather_turned(arrays, axis, dims):
    turned = [jnp.moveaxis(a, dim, 0) for a, dim in zip(arrays, dims)]
    widths = [t[0].size for t in turned]
    both = jnp.concatenate([t.reshape(-1, w) for t, w in zip(turned, widths)], axis=1)
    out = lax.all_gather(both, axis, axis=0, tiled=True)
    tiles = jnp.split(out, [sum(widths[:k]) for k in range(1, len(widths))], axis=1)
    return tuple(
        (
            jnp.moveaxis(b.reshape(-1, *t.shape[1:]), 0, dim)
            for b, t, dim in zip(tiles, turned, dims)
        )
    )


def whole_of(value, axes, dim):
    out = value
    for number in range(len(axes) - 1, -1, -1):
        out = lax.all_gather(out, axes[number], axis=dim, tiled=True)
    return out


def shards(
    w_query,
    low_query,
    high_query,
    w_key,
    low_key,
    high_key,
    w_value,
    low_value,
    high_value,
    w_mixed,
    low_mixed,
    high_mixed,
    norm_train,
    norm_step,
):
    result_query = w_query.astype(jnp.float32) + mix_rate * jnp.dot(
        low_query, high_query, preferred_element_type=jnp.float32
    )
    result_key = w_key.astype(jnp.float32) + mix_rate * jnp.dot(
        low_key, high_key, preferred_element_type=jnp.float32
    )
    result_value = w_value.astype(jnp.float32) + mix_rate * jnp.dot(
        low_value, high_value, preferred_element_type=jnp.float32
    )
    result_mixed = w_mixed.astype(jnp.float32) + mix_rate * jnp.dot(
        low_mixed, high_mixed, preferred_element_type=jnp.float32
    )
    narrow_query, narrow_key, narrow_value, narrow_mixed = (
        result_query.astype(jnp.bfloat16),
        result_key.astype(jnp.bfloat16),
        result_value.astype(jnp.bfloat16),
        result_mixed.astype(jnp.bfloat16),
    )
    final_query, final_key, final_value, final_mixed = gather_turned(
        (narrow_query, narrow_key, narrow_value, narrow_mixed), ROWS, (0, 0, 0, 1)
    )
    serve_norm = whole_of((norm_train + norm_step).astype(jnp.bfloat16), ROWS_TP, 0)
    return (final_query, final_key, final_value, final_mixed, serve_norm)


def solution(mesh):
    finer = Mesh(
        mesh.devices.reshape(8, 4, mesh.shape["tp"], mesh.shape["unit"]),
        ("rows_0", "rows_1", "tp", "unit"),
    )
    return jax.shard_map(
        shards,
        mesh=finer,
        in_specs=(
            P(UNIT_ROWS, "tp"),
            P(UNIT_ROWS, None),
            P("unit", "tp"),
            P(UNIT_ROWS, "tp"),
            P(UNIT_ROWS, None),
            P("unit", "tp"),
            P(UNIT_ROWS, "tp"),
            P(UNIT_ROWS, None),
            P("unit", "tp"),
            P(("unit", "tp"), ROWS),
            P(("unit", "tp"), None),
            P("unit", ROWS),
            P(UNIT_ROWS_TP),
            P(UNIT_ROWS_TP),
        ),
        out_specs=(
            P("unit", "tp"),
            P("unit", "tp"),
            P("unit", "tp"),
            P(("unit", "tp"), None),
            P("unit"),
        ),
        check_vma=False,
    )
```

profile of v0, /device:TPU:2, one launch (start us, length us, event | category | flops | bytes accessed | tf_op | source)
XLA Modules:
  0.0 165.7 jit_solution(15171283167339293376)
XLA Ops:
  7.2 0.0 copy-start
  7.2 0.0 all-gather.2.cloned.1.call-start
  7.2 0.8 copy-done
  8.1 1.2 fusion.4
  9.2 1.0 fusion.8
  10.3 1.0 fusion.7
  11.3 1.2 fusion.2
  12.5 0.8 pad_maximum_fusion
  13.3 0.0 all-gather.2.cloned.1.call-update
  13.3 1.3 dynamic-slice
  14.6 1.3 dynamic-slice.1
  15.8 1.3 dynamic-slice.2
  19.0 0.7 add_convert_fusion
  19.7 0.2 dynamic-update-slice
  19.9 9.9 %all-reduce = bf16[80]{0:T(256)(128)(2,1)S(1)} all-reduce(bf16[80]{0:T(256)(128)(2,1)S(1)} %dynamic-update-slice), channel_id=1, replica_groups=mesh['rows_0'=8,'rows_1'=4,'tp'=4,'unit'=2] {'tp'}, use_global_device_ids=true, to_apply=%add | all-reduce | flops 80 | bytes 320
  29.9 0.2 dynamic-update-slice.1
  30.1 9.4 %all-reduce.1 = bf16[320]{0:T(512)(128)(2,1)S(1)} all-reduce(bf16[320]{0:T(512)(128)(2,1)S(1)} %dynamic-update-slice.1), channel_id=1, replica_groups=mesh['rows_0'=8,'rows_1'=4,'tp'=4,'unit'=2] {'rows_1'}, use_global_device_ids=true, to_apply=%add.1 | all-reduce | flops 320 | bytes 1280
  39.5 0.2 dynamic-update-slice.2
  39.7 20.9 %all-reduce.2 = bf16[2560]{0:T(1024)(128)(2,1)} all-reduce(bf16[2560]{0:T(1024)(128)(2,1)S(1)} %dynamic-update-slice.2), channel_id=1, replica_groups=mesh['rows_0'=8,'rows_1'=4,'tp'=4,'unit'=2] {'rows_0'}, use_global_device_ids=true, to_apply=%add.2 | all-reduce | flops 2560 | bytes 10240
  60.6 77.6 %all-gather.2.cloned.1.call-done = bf16[2560,2560]{1,0:T(8,128)(2,1)} async-done(((bf16[80,2560]{1,0:T(8,128)(2,1)}), bf16[2560,2560]{1,0:T(8,128)(2,1)}) %all-gather.2.cloned.1.call-update) | async-done | bytes 13107216 | tf_op jit(solution)/shard_map/all_gather | solution.py:20
  138.2 9.4 %slice_bitcast_fusion = (bf16[1024,2560]{0,1:T(8,128)(2,1)}, bf16[2560,1024]{1,0:T(8,128)(2,1)}) fusion(bf16[2560,2560]{1,0:T(8,128)(2,1)} %all-gather.2.cloned.1.call-done), kind=kLoop, calls=%fused_computation | loop fusion | bytes 20971520 | tf_op jit(solution)/shard_map/transpose | solution.py:24
  147.6 7.9 %copy.19 = bf16[1024,2560]{1,0:T(8,128)(2,1)} copy(bf16[1024,2560]{0,1:T(8,128)(2,1)} %get-tuple-element.10) | data formatting | bytes 10485760
  155.5 3.4 %fusion.9 = (bf16[2560,256]{1,0:T(8,128)(2,1)}, bf16[2560,256]{1,0:T(8,128)(2,1)}) fusion(bf16[2560,2560]{1,0:T(8,128)(2,1)} %all-gather.2.cloned.1.call-done), kind=kLoop, calls=%fused_computation.16 | loop fusion | bytes 5242880 | tf_op jit(solution)/shard_map/split | solution.py:21
  (3 shorter events, 0.0 us)
Async XLA Ops:
  7.2 0.9 copy-start
  7.2 131.0 %all-gather.2.cloned.1.call-start = ((), (), s32[]{:S(2)}) async-start(), calls=%async_computation | async-start | bytes 13516800 | tf_op jit(solution)/shard_map/all_gather | solution.py:20
Sparse Core Ops, SparseCore 0:
  13.4 124.7 all-gather.1
where the time goes:
time: 166 us
  waiting for transfers between devices  77.6 us (47%)
  blocking collectives  40.2 us (24%)
  local copies, waits for them, and re-layouts  26 us (16%)
  between operations  16 us (10%)
  matrix products  4.39 us (3%)
    all_gather x1, waiting for transfers between devices, gather_turned(): out = lax.all_gather(both, axis, axis=0, tiled=True)  77.6 us
    unnamed x3, blocking collectives  40.2 us
    unnamed x12, local copies, waits for them, and re-layouts  13.3 us
    transpose x1, local copies, waits for them, and re-layouts, gather_turned(): jnp.moveaxis(b.reshape(-1, *t.shape[1:]), 0, dim)  9.4 us
    split x1, local copies, waits for them, and re-layouts, gather_turned(): jnp.split(out, [sum(widths[:k]) for k in range(1, len(widths))], axis=1)  3.38 us
  transfers between devices with their start and end apart: 1, of which 1 were waited for; matrix products, arithmetic and copies ran while one was open for 3% of the time, Pallas kernels for 0%

commit v1 on v0

v1 whole, which is shorter than its diff:
```python
import functools
import heapq

import jax
import jax.numpy as jnp
from jax import lax
from jax.experimental import pallas as pl
from jax.experimental.pallas import tpu as pltpu
from jax.sharding import PartitionSpec as P

MESH = pl.DeviceIdType.MESH
UNIT_ROWS = ("unit", "rows")
UNIT_ROWS_TP = ("unit", "rows", "tp")

mix_rate = 0.5

NY, NZ = 4, 8
SIZE = {"y": NY, "z": NZ}
LINKS = (("y", 1), ("y", -1), ("z", 1), ("z", -1))
RATE, LATENCY, LEAD = 46.6e3, 2.0, 3.0


def reach(n, step, side):
    return n // 2 if (side == 0) == (step > 0) else n - 1 - n // 2


def onward(piece, via, hops):
    first, second = ("y", "z") if piece["y_first"] else ("z", "y")
    if via is None:
        out = [((axis, step), 1) for axis in (first, second) for step in (1, -1)]
    else:
        out = [(via, hops + 1)]
        if via[0] == first:
            out += [((second, step), 1) for step in (1, -1)]
    return [(l, h) for l, h in out if h <= reach(SIZE[l[0]], l[1], piece["side"])]


def plan(pieces):
    def urgency(piece, link, hops):
        left = reach(SIZE[link[0]], link[1], piece["side"]) - hops
        first, second = ("y", "z") if piece["y_first"] else ("z", "y")
        return piece["phase"], -(left + (SIZE[second] // 2 if link[0] == first else 0))

    queue, free, seq = {l: [] for l in LINKS}, dict.fromkeys(LINKS, 0.0), 0
    events, steps, got, last = [], [], {}, dict.fromkeys(LINKS, 0.0)

    def hold(k, origin, via, hops):
        nonlocal seq
        for link, h in onward(pieces[k], via, hops):
            seq += 1
            heapq.heappush(queue[link], (urgency(pieces[k], link, h), seq, k, origin, h))

    for k in range(len(pieces)):
        got[k, (0, 0)] = 0.0
        hold(k, (0, 0), None, 0)
    now = 0.0
    while True:
        for link in LINKS:
            if free[link] <= now + 1e-9 and queue[link]:
                _, _, k, origin, h = heapq.heappop(queue[link])
                issue = max(got[k, origin], now - LEAD, last[link])
                last[link] = issue
                seq += 1
                steps.append((issue, seq, "send", k, origin, link))
                free[link] = now + pieces[k]["bytes"] / RATE
                dy, dz = origin
                there = ((dy - link[1]) % NY, dz) if link[0] == "y" else (dy, (dz - link[1]) % NZ)
                heapq.heappush(events, (free[link], seq, None))
                heapq.heappush(events, (free[link] + LATENCY, seq, (k, there, link, h)))
        if not events:
            break
        now = events[0][0]
        while events and events[0][0] <= now + 1e-9:
            _, _, landed = heapq.heappop(events)
            if landed is not None:
                k, origin, link, h = landed
                got[k, origin] = now
                seq += 1
                steps.append((now, seq, "wait", k, origin, link))
                hold(k, origin, link, h)
    steps.sort(key=lambda s: (s[0], s[2] == "send", s[1]))
    return [(t, *rest) for t, _, *rest in steps]


def make_pieces(depth, mixed, rest):
    pieces = []
    for phase, buffer, columns in ((0, "mixed", mixed), (1, "rest", rest)):
        cut = depth * 2 // 5 // 16 * 16
        for y_first, low, count in ((True, 0, cut), (False, cut, depth - cut)):
            for side in (0, 1):
                pieces.append(
                    dict(
                        phase=phase,
                        buffer=buffer,
                        y_first=y_first,
                        side=side,
                        row=low,
                        rows=count,
                        col=side * columns // 2,
                        cols=columns // 2,
                        bytes=count * columns,
                    )
                )
    return pieces


def merged(w, low_t, high):
    product = lax.dot_general(
        low_t, high, (((0,), (0,)), ((), ())), preferred_element_type=jnp.float32
    )
    return (w.astype(jnp.float32) + mix_rate * product).astype(jnp.bfloat16)


def gather_kernel(
    n_tp,
    depth,
    w_query,
    low_query,
    high_query,
    w_key,
    low_key,
    high_key,
    w_value,
    low_value,
    high_value,
    w_mixed,
    low_mixed,
    high_mixed,
    norm_train,
    norm_step,
    rest,
    mixed_out,
    norm_out,
    mixed,
    peers,
    norms,
    sent,
    got,
    sent_norm,
    got_norm,
):
    rows, t = lax.axis_index("rows"), lax.axis_index("tp")
    z, y = rows // NY, lax.rem(rows, NY)
    ys = [lax.rem(y + d, NY) for d in range(NY)]
    zs = [lax.rem(z + d, NZ) for d in range(NZ)]
    ts = [lax.rem(t + d, n_tp) for d in range(n_tp)]
    at = {(dy, dz): zs[dz] * NY + ys[dy] for dy in range(NY) for dz in range(NZ)}
    to = {
        ("y", 1): at[1, 0],
        ("y", -1): at[NY - 1, 0],
        ("z", 1): at[0, 1],
        ("z", -1): at[0, NZ - 1],
    }

    barrier = pltpu.get_barrier_semaphore()
    for link in LINKS:
        pl.semaphore_signal(barrier, 1, device_id={"rows": to[link]}, device_id_type=MESH)
    for d in range(1, n_tp):
        pl.semaphore_signal(barrier, 1, device_id={"tp": ts[d]}, device_id_type=MESH)

    mine = pl.ds(pl.multiple_of(rows * depth, 16), depth)
    q, k = w_query.shape[1], w_key.shape[1]
    mixed[mine, :] = merged(w_mixed[...], high_mixed[...], low_mixed[...])
    rest[mine, :q] = merged(w_query[...], low_query[...], high_query[...])
    rest[mine, q : q + k] = merged(w_key[...], low_key[...], high_key[...])
    rest[mine, q + k :] = merged(w_value[...], low_value[...], high_value[...])
    share = norm_train.shape[1]
    gain = norm_train[...] + norm_step[...]
    wide = jnp.concatenate([gain, jnp.zeros((1, 128 - share), jnp.float32)], axis=1)
    peers[t] = pltpu.roll(wide, t * share, 1)

    pl.semaphore_wait(barrier, len(LINKS) + n_tp - 1)

    buffers = {"mixed": mixed, "rest": rest}
    pieces = make_pieces(depth, mixed.shape[1], rest.shape[1])

    def copy(k, origin, link):
        p, r = pieces[k], at[origin]
        ref = buffers[p["buffer"]].at[
            pl.ds(pl.multiple_of(r * depth + p["row"], 16), p["rows"]),
            pl.ds(p["col"], p["cols"]),
        ]
        return pltpu.make_async_remote_copy(
            src_ref=ref,
            dst_ref=ref,
            send_sem=sent.at[p["phase"]],
            recv_sem=got.at[k, r],
            device_id={"rows": to[link]},
            device_id_type=MESH,
        )

    def norm_copy(ref, n, axis, index):
        return pltpu.make_async_remote_copy(
            src_ref=ref,
            dst_ref=ref,
            send_sem=sent_norm.at[n],
            recv_sem=got_norm.at[n],
            device_id={axis: index},
            device_id_type=MESH,
        )

    def peer_copy(d):
        return norm_copy(peers.at[t], d - 1, "tp", ts[d])

    def y_copy(n):
        dy, link = ((0, ("y", 1)), (0, ("y", -1)), (NY - 1, ("y", 1)))[n]
        return norm_copy(norms.at[pl.ds(at[dy, 0], 1)], 3 + n, "rows", to[link])

    def z_copy(n):
        dz, link = (-n % NZ, ("z", 1)) if n < 4 else (n - 4, ("z", -1))
        return norm_copy(norms.at[pl.ds(zs[dz] * NY, NY)], 6 + n, "rows", to[link])

    def norm_step_0():
        for d in range(1, n_tp):
            peer_copy(d).start()

    def norm_step_1():
        for d in range(1, n_tp):
            peer_copy(d).wait_recv()
        norms[rows] = sum(peers[d] for d in range(n_tp))

    def norm_step_2():
        y_copy(0).start()
        y_copy(1).start()

    def norm_step_3():
        y_copy(0).wait_recv()
        y_copy(2).start()
        y_copy(1).wait_recv()

    def norm_step_4():
        y_copy(2).wait_recv()
        z_copy(0).start()
        z_copy(4).start()

    def norm_hop(n):
        z_copy(n - 1).wait_recv()
        z_copy(n).start()
        if n < 3:
            z_copy(n + 3).wait_recv()
            z_copy(n + 4).start()

    def norm_last():
        z_copy(3).wait_recv()
        z_copy(6).wait_recv()
        n_norm = norms.shape[0] * share * n_tp
        lane = lax.broadcasted_iota(jnp.int32, (1, 128), 1)
        lines = [jnp.zeros((1, 128), jnp.float32) for _ in range(n_norm // 128)]
        width = share * n_tp
        for r in range(norms.shape[0]):
            line, off = divmod(r * width, 128)
            part = pltpu.roll(norms[r], off, 1) if off else norms[r]
            lines[line] += jnp.where(lane >= off, part, 0.0)
            if off + width > 128:
                lines[line + 1] += jnp.where(lane < off + width - 128, part, 0.0)
        norm_out[...] = jnp.concatenate(lines, axis=0).astype(norm_out.dtype)

    def turn(j):
        part = mixed[128 * j : 128 * (j + 1), :]
        mixed_out[:, 128 * j : 128 * (j + 1)] = part.T

    steps = plan(pieces)
    turned = [s[0] for s in steps if s[1] == "wait" and pieces[s[2]]["phase"] == 0][-1]
    end = steps[-1][0]
    n_turn = mixed.shape[0] // 128
    side_jobs = [(0.5, norm_step_0), (6.0, norm_step_1), (8.0, norm_step_2), (14.0, norm_step_3)]
    side_jobs += [(20.0, norm_step_4)]
    side_jobs += [(20.0 + 6.0 * n, functools.partial(norm_hop, n)) for n in range(1, 4)]
    side_jobs += [(46.0, norm_last)]
    gap = (end - 8.0 - turned) / n_turn
    side_jobs += [
        (turned + 0.01 + gap * j, functools.partial(turn, j)) for j in range(n_turn)
    ]
    side_jobs.sort(key=lambda job: job[0])

    for when, what, k, origin, link in steps:
        while side_jobs and side_jobs[0][0] < when:
            side_jobs.pop(0)[1]()
        if what == "wait":
            copy(k, origin, link).wait_recv()
        else:
            copy(k, origin, link).start()
    for _, job in side_jobs:
        job()

    n_rows = mixed.shape[0]
    for phase, buffer in ((0, mixed), (1, rest)):
        others = buffer.at[pl.ds(0, n_rows - depth)]
        pltpu.make_async_remote_copy(
            src_ref=others,
            dst_ref=others,
            send_sem=sent.at[phase],
            recv_sem=got.at[0, 0],
            device_id={"rows": to["y", 1]},
            device_id_type=MESH,
        ).wait_send()
    for d in range(1, n_tp):
        peer_copy(d).wait_send()
    for n in range(3):
        y_copy(n).wait_send()
    for n in range(7):
        z_copy(n).wait_send()


def put_kernel(rest, mixed, final_query, final_key, final_value, final_mixed, sems):
    q, k = final_query.shape[1], final_key.shape[1]
    copies = [
        pltpu.make_async_copy(mixed, final_mixed, sems.at[0]),
        pltpu.make_async_copy(rest.at[:, pl.ds(0, q)], final_query, sems.at[1]),
        pltpu.make_async_copy(rest.at[:, pl.ds(q, k)], final_key, sems.at[2]),
        pltpu.make_async_copy(rest.at[:, pl.ds(q + k, k)], final_value, sems.at[3]),
    ]
    for c in copies:
        c.start()
    for c in copies:
        c.wait()


def shards(n_rows, n_tp, *args):
    (
        w_query,
        low_query,
        high_query,
        w_key,
        low_key,
        high_key,
        w_value,
        low_value,
        high_value,
        w_mixed,
        low_mixed,
        high_mixed,
        norm_train,
        norm_step,
    ) = args
    depth, q, k = w_query.shape[0], w_query.shape[1], w_key.shape[1]
    m = w_mixed.shape[0]
    total = n_rows * depth
    n_norm = n_rows * n_tp * norm_train.shape[0]
    bf16, f32 = jnp.bfloat16, jnp.float32
    vmem = pl.BlockSpec(memory_space=pltpu.VMEM)
    n_pieces = len(make_pieces(depth, m, q + 2 * k))
    rest, mixed, norm = pl.pallas_call(
        functools.partial(gather_kernel, n_tp, depth),
        out_shape=(
            pltpu.VMEM((total, q + 2 * k), bf16),
            pltpu.VMEM((m, total), bf16),
            jax.ShapeDtypeStruct((n_norm // 128, 128), bf16),
        ),
        in_specs=[vmem] * 14,
        out_specs=(vmem, vmem, vmem),
        scratch_shapes=[
            pltpu.VMEM((total, m), bf16),
            pltpu.VMEM((n_tp, 1, 128), f32),
            pltpu.VMEM((n_rows, 1, 128), f32),
            pltpu.SemaphoreType.DMA((2,)),
            pltpu.SemaphoreType.DMA((n_pieces, n_rows)),
            pltpu.SemaphoreType.DMA((13,)),
            pltpu.SemaphoreType.DMA((13,)),
        ],
        compiler_params=pltpu.CompilerParams(
            collective_id=0, has_side_effects=True, vmem_limit_bytes=40 << 20
        ),
        name="gather",
    )(
        w_query,
        low_query.T,
        high_query,
        w_key,
        low_key.T,
        high_key,
        w_value,
        low_value.T,
        high_value,
        w_mixed.T,
        low_mixed.T,
        high_mixed,
        norm_train.reshape(1, -1),
        norm_step.reshape(1, -1),
    )
    hbm = pl.BlockSpec(memory_space=pltpu.HBM)
    final_query, final_key, final_value, final_mixed = pl.pallas_call(
        put_kernel,
        out_shape=(
            jax.ShapeDtypeStruct((total, q), bf16),
            jax.ShapeDtypeStruct((total, k), bf16),
            jax.ShapeDtypeStruct((total, k), bf16),
            jax.ShapeDtypeStruct((m, total), bf16),
        ),
        in_specs=[vmem] * 2,
        out_specs=(hbm,) * 4,
        scratch_shapes=[pltpu.SemaphoreType.DMA((4,))],
        name="put",
    )(rest, mixed)
    return final_query, final_key, final_value, final_mixed, norm.reshape(-1)


def solution(mesh):
    return jax.shard_map(
        functools.partial(shards, mesh.shape["rows"], mesh.shape["tp"]),
        mesh=mesh,
        in_specs=(
            P(UNIT_ROWS, "tp"),
            P(UNIT_ROWS, None),
            P("unit", "tp"),
            P(UNIT_ROWS, "tp"),
            P(UNIT_ROWS, None),
            P("unit", "tp"),
            P(UNIT_ROWS, "tp"),
            P(UNIT_ROWS, None),
            P("unit", "tp"),
            P(("unit", "tp"), "rows"),
            P(("unit", "tp"), None),
            P("unit", "rows"),
            P(UNIT_ROWS_TP),
            P(UNIT_ROWS_TP),
        ),
        out_specs=(
            P("unit", "tp"),
            P("unit", "tp"),
            P("unit", "tp"),
            P(("unit", "tp"), None),
            P("unit"),
        ),
        check_vma=False,
    )
```

time: 166 us -> 109 us (0.66)
  Pallas kernels: 0 us -> 91.1 us
  waiting for transfers between devices: 77.6 us -> 0 us
  blocking collectives: 40.2 us -> 0 us
  between operations: 16 us -> 0.68 us
  local copies, waits for them, and re-layouts: 26 us -> 16.9 us
  matrix products: 4.39 us -> 0 us
    pallas_call x0 -> x2, Pallas kernels: none -> 91.1 us  [the longest x1 81.6 us: shards(): pl.pallas_call(functools.partial(gather_kernel, n_tp, depth), out_shape=(...]
    all_gather x1 -> x0, waiting for transfers between devices: 77.6 us -> none  [gather_turned(): out = lax.all_gather(both, axis, axis=0, tiled=True)]
    unnamed x3 -> x0, blocking collectives: 40.2 us -> none
    transpose x1 -> x0, local copies, waits for them, and re-layouts: 9.4 us -> none  [gather_turned(): jnp.moveaxis(b.reshape(-1, *t.shape[1:]), 0, dim)]
    dot_general x4 -> x0, matrix products: 4.39 us -> none  [the longest x1 1.22 us: shards(): jnp.dot(low_query, high_query, preferred_element_type=jnp.float32)]
    unnamed x12 -> x33, local copies, waits for them, and re-layouts: 13.3 us -> 16.9 us
    split x1 -> x0, local copies, waits for them, and re-layouts: 3.38 us -> none  [gather_turned(): jnp.split(out, [sum(widths[:k]) for k in range(1, len(widths))], axis=1)]
  transfers between devices with their start and end apart: 1 -> 0, of which waited for: 1 -> 0; matrix products, arithmetic and copies ran while one was open for 3% -> 0% of each run, Pallas kernels for 0% -> 0%
where the time goes in v1:
time: 109 us
  Pallas kernels  91.1 us (84%)
  local copies, waits for them, and re-layouts  16.9 us (16%)
    pallas_call x1, Pallas kernels, shards(): pl.pallas_call(functools.partial(gather_kernel, n_tp, depth), out_shape=(...  81.6 us
    unnamed x33, local copies, waits for them, and re-layouts  16.9 us
    pallas_call x1, Pallas kernels, shards(): pl.pallas_call(put_kernel, out_shape=(jax.ShapeDtypeStruct((total, q), bf...  9.51 us

profile of v1, /device:TPU:2, one launch (start us, length us, event | category | flops | bytes accessed | tf_op | source)
XLA Modules:
  0.0 108.7 jit_solution(6242961696381505286)
XLA Ops:
  0.6 0.0 copy-start.2
  0.6 0.9 copy-done.2
  1.6 0.9 copy-done.3
  2.5 0.0 copy-start.4
  2.5 0.9 copy-done.4
  3.4 0.0 copy-start.5
  3.4 0.9 copy-done.5
  4.3 0.0 copy-start.6
  4.3 0.8 copy-done.6
  5.1 0.0 copy-start.7
  5.1 0.8 copy-done.7
  5.8 0.0 copy-start.8
  5.8 0.8 copy-done.8
  6.6 0.0 copy-start.9
  6.6 0.8 copy-done.9
  7.4 0.0 copy-start.10
  7.4 0.7 copy-done.10
  8.1 0.0 copy-start.11
  8.1 0.7 copy-done.11
  8.8 0.0 copy-start.12
  8.8 0.7 copy-done.12
  9.5 0.0 copy-start.13
  9.5 0.7 copy-done.13
  10.2 0.0 copy-start.14
  10.2 0.7 copy-done.14
  10.9 0.7 copy-done.15
  11.5 81.6 %gather.1 = (bf16[2560,1536]{1,0:T(8,128)(2,1)S(1)}, bf16[1024,2560]{1,0:T(8,128)(2,1)S(1)}, bf16[20,128]{1,0:T(8,128)(2,1)S(1)}) custom-call(bf16[80,1024]{1,0:T(8,128)(2,1)S(1)} %copy-done.2, bf16[64,80]{1,0:T(8,128)(2,1)S(1)} %bitcast.10, bf16[64,1024]{1,0:T(8,128)(2,1)S(1)} %copy-done.4, bf16[80,256]{1,0:T(8,128)(2,1)S(1)} %copy-done.6, ...), custom_call_target="tpu_custom_call" | custom-call | tf_op jit(solution)/shard_map/gather/pallas_call | solution.py:343
  93.2 0.0 copy-start
  93.2 3.0 %copy-done = bf16[2560,1536]{1,0:T(8,128)(2,1)} copy-done((bf16[2560,1536]{1,0:T(8,128)(2,1)}, bf16[2560,1536]{1,0:T(8,128)(2,1)S(1)}, u32[]{:S(2)}) %copy-start) | copy-done | bytes 7864344
  96.2 2.4 %copy-done.1 = bf16[1024,2560]{1,0:T(8,128)(2,1)} copy-done((bf16[1024,2560]{1,0:T(8,128)(2,1)}, bf16[1024,2560]{1,0:T(8,128)(2,1)S(1)}, u32[]{:S(2)}) %copy-start.1) | copy-done | bytes 5242904
  98.6 9.5 %put.1 = (bf16[2560,1024]{1,0:T(8,128)(2,1)}, bf16[2560,256]{1,0:T(8,128)(2,1)}, bf16[2560,256]{1,0:T(8,128)(2,1)}, bf16[1024,2560]{1,0:T(8,128)(2,1)}) custom-call(bf16[2560,1536]{1,0:T(8,128)(2,1)} %copy-done, bf16[1024,2560]{1,0:T(8,128)(2,1)} %copy-done.1), custom_call_target="tpu_custom_call" | custom-call | tf_op jit(solution)/shard_map/put/pallas_call | solution.py:382
  108.1 0.6 copy.20
  (3 shorter events, 0.0 us)
Async XLA Ops:
  0.6 0.9 copy-start.2
  1.6 0.9 copy-start.3
  2.5 0.9 copy-start.4
  3.4 0.9 copy-start.5
  4.3 0.8 copy-start.6
  5.1 0.8 copy-start.7
  5.8 0.8 copy-start.8
  6.6 0.8 copy-start.9
  7.4 0.7 copy-start.10
  8.1 0.7 copy-start.11
  8.8 0.7 copy-start.12
  9.5 0.7 copy-start.13
  10.2 0.7 copy-start.14
  10.9 0.7 copy-start.15
  93.2 3.0 %copy-start = (bf16[2560,1536]{1,0:T(8,128)(2,1)}, bf16[2560,1536]{1,0:T(8,128)(2,1)S(1)}, u32[]{:S(2)}) copy-start(bf16[2560,1536]{1,0:T(8,128)(2,1)S(1)} %get-tuple-element.12.rest) | copy-start | bytes 23592964
  96.2 2.4 %copy-start.1 = (bf16[1024,2560]{1,0:T(8,128)(2,1)}, bf16[1024,2560]{1,0:T(8,128)(2,1)S(1)}, u32[]{:S(2)}) copy-start(bf16[1024,2560]{1,0:T(8,128)(2,1)S(1)} %get-tuple-element.13.mixed) | copy-start | bytes 15728644

commit v2 on v1

--- a/solution.py
+++ b/solution.py
@@ -13,6 +13,7 @@
 UNIT_ROWS_TP = ("unit", "rows", "tp")
 
 mix_rate = 0.5
+N_ARGS = 14
 
 NY, NZ = 4, 8
 SIZE = {"y": NY, "z": NZ}
@@ -111,34 +112,21 @@
     return (w.astype(jnp.float32) + mix_rate * product).astype(jnp.bfloat16)
 
 
-def gather_kernel(
-    n_tp,
-    depth,
-    w_query,
-    low_query,
-    high_query,
-    w_key,
-    low_key,
-    high_key,
-    w_value,
-    low_value,
-    high_value,
-    w_mixed,
-    low_mixed,
-    high_mixed,
-    norm_train,
-    norm_step,
-    rest,
-    mixed_out,
-    norm_out,
-    mixed,
-    peers,
-    norms,
-    sent,
-    got,
-    sent_norm,
-    got_norm,
-):
+def gather_kernel(n_tp, depth, *refs):
+    given, (rest, mixed_out, norm_out), held = refs[:N_ARGS], refs[N_ARGS : N_ARGS + 3], refs[N_ARGS + 3 :]
+    fetched, (mixed, peers, norms, fetch_sem, sent, got, sent_norm, got_norm) = (
+        held[:N_ARGS],
+        held[N_ARGS:],
+    )
+    w_query, low_query, high_query, w_key, low_key, high_key, w_value, low_value, high_value = fetched[:9]
+    w_mixed, low_mixed, high_mixed, norm_train, norm_step = fetched[9:]
+    fetches = [
+        pltpu.make_async_copy(a, b, fetch_sem.at[n])
+        for n, (a, b) in enumerate(zip(given, fetched))
+    ]
+    for n in (*range(9, N_ARGS), *range(9)):
+        fetches[n].start()
+
     rows, t = lax.axis_index("rows"), lax.axis_index("tp")
     z, y = rows // NY, lax.rem(rows, NY)
     ys = [lax.rem(y + d, NY) for d in range(NY)]
@@ -160,14 +148,20 @@
 
     mine = pl.ds(pl.multiple_of(rows * depth, 16), depth)
     q, k = w_query.shape[1], w_key.shape[1]
+    for n in range(9, N_ARGS):
+        fetches[n].wait()
     mixed[mine, :] = merged(w_mixed[...], high_mixed[...], low_mixed[...])
-    rest[mine, :q] = merged(w_query[...], low_query[...], high_query[...])
-    rest[mine, q : q + k] = merged(w_key[...], low_key[...], high_key[...])
-    rest[mine, q + k :] = merged(w_value[...], low_value[...], high_value[...])
     share = norm_train.shape[1]
     gain = norm_train[...] + norm_step[...]
     wide = jnp.concatenate([gain, jnp.zeros((1, 128 - share), jnp.float32)], axis=1)
     peers[t] = pltpu.roll(wide, t * share, 1)
+
+    def merge_rest():
+        for n in range(9):
+            fetches[n].wait()
+        rest[mine, :q] = merged(w_query[...], low_query[...], high_query[...])
+        rest[mine, q : q + k] = merged(w_key[...], low_key[...], high_key[...])
+        rest[mine, q + k :] = merged(w_value[...], low_value[...], high_value[...])
 
     pl.semaphore_wait(barrier, len(LINKS) + n_tp - 1)
 
@@ -271,15 +265,16 @@
     side_jobs += [
         (turned + 0.01 + gap * j, functools.partial(turn, j)) for j in range(n_turn)
     ]
+    side_jobs += [(min(s[0] for s in steps if pieces[s[2]]["phase"]) - 0.01, merge_rest)]
     side_jobs.sort(key=lambda job: job[0])
 
-    for when, what, k, origin, link in steps:
+    for when, what, piece, origin, link in steps:
         while side_jobs and side_jobs[0][0] < when:
             side_jobs.pop(0)[1]()
         if what == "wait":
-            copy(k, origin, link).wait_recv()
+            copy(piece, origin, link).wait_recv()
         else:
-            copy(k, origin, link).start()
+            copy(piece, origin, link).start()
     for _, job in side_jobs:
         job()
 
@@ -302,14 +297,20 @@
         z_copy(n).wait_send()
 
 
-def put_kernel(rest, mixed, final_query, final_key, final_value, final_mixed, sems):
+def put_kernel(rest, mixed, norm, final_query, final_key, final_value, final_mixed, serve_norm, sems):
     q, k = final_query.shape[1], final_key.shape[1]
-    copies = [
-        pltpu.make_async_copy(mixed, final_mixed, sems.at[0]),
-        pltpu.make_async_copy(rest.at[:, pl.ds(0, q)], final_query, sems.at[1]),
-        pltpu.make_async_copy(rest.at[:, pl.ds(q, k)], final_key, sems.at[2]),
-        pltpu.make_async_copy(rest.at[:, pl.ds(q + k, k)], final_value, sems.at[3]),
-    ]
+    moves = [(norm, serve_norm)]
+    for source, final, cuts in (
+        (mixed, final_mixed, 4),
+        (rest.at[:, pl.ds(0, q)], final_query, 4),
+        (rest.at[:, pl.ds(q, k)], final_key, 2),
+        (rest.at[:, pl.ds(q + k, k)], final_value, 2),
+    ):
+        count = final.shape[0] // cuts
+        for c in range(cuts):
+            part = pl.ds(c * count, count)
+            moves.append((source.at[part], final.at[part]))
+    copies = [pltpu.make_async_copy(a, b, sems.at[n]) for n, (a, b) in enumerate(moves)]
     for c in copies:
         c.start()
     for c in copies:
@@ -340,29 +341,8 @@
     bf16, f32 = jnp.bfloat16, jnp.float32
     vmem = pl.BlockSpec(memory_space=pltpu.VMEM)
     n_pieces = len(make_pieces(depth, m, q + 2 * k))
-    rest, mixed, norm = pl.pallas_call(
-        functools.partial(gather_kernel, n_tp, depth),
-        out_shape=(
-            pltpu.VMEM((total, q + 2 * k), bf16),
-            pltpu.VMEM((m, total), bf16),
-            jax.ShapeDtypeStruct((n_norm // 128, 128), bf16),
-        ),
-        in_specs=[vmem] * 14,
-        out_specs=(vmem, vmem, vmem),
-        scratch_shapes=[
-            pltpu.VMEM((total, m), bf16),
-            pltpu.VMEM((n_tp, 1, 128), f32),
-            pltpu.VMEM((n_rows, 1, 128), f32),
-            pltpu.SemaphoreType.DMA((2,)),
-            pltpu.SemaphoreType.DMA((n_pieces, n_rows)),
-            pltpu.SemaphoreType.DMA((13,)),
-            pltpu.SemaphoreType.DMA((13,)),
-        ],
-        compiler_params=pltpu.CompilerParams(
-            collective_id=0, has_side_effects=True, vmem_limit_bytes=40 << 20
-        ),
-        name="gather",
-    )(
+    hbm = pl.BlockSpec(memory_space=pltpu.HBM)
+    given = (
         w_query,
         low_query.T,
         high_query,
@@ -378,21 +358,47 @@
         norm_train.reshape(1, -1),
         norm_step.reshape(1, -1),
     )
-    hbm = pl.BlockSpec(memory_space=pltpu.HBM)
-    final_query, final_key, final_value, final_mixed = pl.pallas_call(
+    made = pl.pallas_call(
+        functools.partial(gather_kernel, n_tp, depth),
+        out_shape=(
+            pltpu.VMEM((total, q + 2 * k), bf16),
+            pltpu.VMEM((m, total), bf16),
+            pltpu.VMEM((n_norm // 128, 128), bf16),
+        ),
+        in_specs=[hbm] * N_ARGS,
+        out_specs=(vmem, vmem, vmem),
+        scratch_shapes=[
+            *(pltpu.VMEM(a.shape, a.dtype) for a in given),
+            pltpu.VMEM((total, m), bf16),
+            pltpu.VMEM((n_tp, 1, 128), f32),
+            pltpu.VMEM((n_rows, 1, 128), f32),
+            pltpu.SemaphoreType.DMA((N_ARGS,)),
+            pltpu.SemaphoreType.DMA((2,)),
+            pltpu.SemaphoreType.DMA((n_pieces, n_rows)),
+            pltpu.SemaphoreType.DMA((13,)),
+            pltpu.SemaphoreType.DMA((13,)),
+        ],
+        compiler_params=pltpu.CompilerParams(
+            collective_id=0, has_side_effects=True, vmem_limit_bytes=16 << 20
+        ),
+        name="gather",
+    )(*(pltpu.with_memory_space_constraint(a, pltpu.HBM) for a in given))
+    final_query, final_key, final_value, final_mixed, serve_norm = pl.pallas_call(
         put_kernel,
         out_shape=(
             jax.ShapeDtypeStruct((total, q), bf16),
             jax.ShapeDtypeStruct((total, k), bf16),
             jax.ShapeDtypeStruct((total, k), bf16),
             jax.ShapeDtypeStruct((m, total), bf16),
+            jax.ShapeDtypeStruct((n_norm // 128, 128), bf16),
         ),
-        in_specs=[vmem] * 2,
-        out_specs=(hbm,) * 4,
-        scratch_shapes=[pltpu.SemaphoreType.DMA((4,))],
+        in_specs=[vmem] * 3,
+        out_specs=(hbm,) * 5,
+        scratch_shapes=[pltpu.SemaphoreType.DMA((13,))],
+        compiler_params=pltpu.CompilerParams(vmem_limit_bytes=2 << 20),
         name="put",
-    )(rest, mixed)
-    return final_query, final_key, final_value, final_mixed, norm.reshape(-1)
+    )(*(pltpu.with_memory_space_constraint(a, pltpu.VMEM) for a in made))
+    return final_query, final_key, final_value, final_mixed, serve_norm.reshape(-1)
 
 
 def solution(mesh):

time: 109 us -> 87.4 us (0.80)
  local copies, waits for them, and re-layouts: 16.9 us -> 0 us
  Pallas kernels: 91.1 us -> 86.7 us
    unnamed x33 -> x0, local copies, waits for them, and re-layouts: 16.9 us -> none
    pallas_call x1, Pallas kernels: 9.51 us -> 4.85 us  [shards(): pl.pallas_call(put_kernel, out_shape=(jax.ShapeDtypeStruct((total, q), bf...]
where the time goes in v2:
time: 87.4 us; the launch traced here: 87.3 us
  Pallas kernels  86.7 us (99%)
    pallas_call x1, Pallas kernels, shards(): pl.pallas_call(functools.partial(gather_kernel, n_tp, depth), out_shape=(...  81.8 us
    pallas_call x1, Pallas kernels, shards(): pl.pallas_call(put_kernel, out_shape=(jax.ShapeDtypeStruct((total, q), bf...  4.85 us

profile of v2, /device:TPU:2, one launch (start us, length us, event | category | flops | bytes accessed | tf_op | source)
XLA Modules:
  0.0 87.3 jit_solution(532289898720988922)
XLA Ops:
  0.6 81.8 %gather.1 = (bf16[2560,1536]{1,0:T(8,128)(2,1)S(1)}, bf16[1024,2560]{1,0:T(8,128)(2,1)S(1)}, bf16[20,128]{1,0:T(8,128)(2,1)S(1)}) custom-call(bf16[80,1024]{1,0:T(8,128)(2,1)} %refs_0_.1, bf16[64,80]{1,0:T(8,128)(2,1)} %bitcast.10, bf16[64,1024]{1,0:T(8,128)(2,1)} %refs_2_.1, bf16[80,256]{1,0:T(8,128)(2,1)} %refs_3_.1, bf16[64,80]{1,0:T(8,128)(2,1)} %bitcast.11, ...), custom_call_target="tpu_custom_call" | custom-call | tf_op jit(solution)/shard_map/gather/pallas_call | solution.py:361
  82.5 4.8 %put.1 = (bf16[2560,1024]{1,0:T(8,128)(2,1)}, bf16[2560,256]{1,0:T(8,128)(2,1)}, bf16[2560,256]{1,0:T(8,128)(2,1)}, bf16[1024,2560]{1,0:T(8,128)(2,1)}, bf16[20,128]{1,0:T(8,128)(2,1)}) custom-call(bf16[2560,1536]{1,0:T(8,128)(2,1)S(1)} %get-tuple-element.13.rest, bf16[1024,2560]{1,0:T(8,128)(2,1)S(1)} %get-tuple-element.14.mixed, ...), custom_call_target="tpu_custom_call" | custom-call | tf_op jit(solution)/shard_map/put/pallas_call | solution.py:386

commit v3 on v2

--- a/solution.py
+++ b/solution.py
@@ -18,7 +18,7 @@
 NY, NZ = 4, 8
 SIZE = {"y": NY, "z": NZ}
 LINKS = (("y", 1), ("y", -1), ("z", 1), ("z", -1))
-RATE, LATENCY, LEAD = 46.6e3, 2.0, 3.0
+RATE, LATENCY, LEAD = 46.6e3, 5.0, 6.0
 
 
 def reach(n, step, side):

time: 87.4 us -> 86.4 us (0.989)
  Pallas kernels: 86.7 us -> 85.7 us
    pallas_call x1, Pallas kernels: 81.8 us -> 80.8 us  [shards(): pl.pallas_call(functools.partial(gather_kernel, n_tp, depth), out_shape=(...]
where the time goes in v3:
time: 86.4 us; the launch traced here: 86.3 us
  Pallas kernels  85.7 us (99%)
    pallas_call x1, Pallas kernels, shards(): pl.pallas_call(functools.partial(gather_kernel, n_tp, depth), out_shape=(...  80.8 us
    pallas_call x1, Pallas kernels, shards(): pl.pallas_call(put_kernel, out_shape=(jax.ShapeDtypeStruct((total, q), bf...  4.85 us

profile of v3, /device:TPU:2, one launch (start us, length us, event | category | flops | bytes accessed | tf_op | source)
XLA Modules:
  0.0 86.3 jit_solution(7369731086508042674)
XLA Ops:
  0.6 80.8 %gather.1 = (bf16[2560,1536]{1,0:T(8,128)(2,1)S(1)}, bf16[1024,2560]{1,0:T(8,128)(2,1)S(1)}, bf16[20,128]{1,0:T(8,128)(2,1)S(1)}) custom-call(bf16[80,1024]{1,0:T(8,128)(2,1)} %refs_0_.1, bf16[64,80]{1,0:T(8,128)(2,1)} %bitcast.10, bf16[64,1024]{1,0:T(8,128)(2,1)} %refs_2_.1, bf16[80,256]{1,0:T(8,128)(2,1)} %refs_3_.1, bf16[64,80]{1,0:T(8,128)(2,1)} %bitcast.11, ...), custom_call_target="tpu_custom_call" | custom-call | tf_op jit(solution)/shard_map/gather/pallas_call | solution.py:361
  81.4 4.8 %put.1 = (bf16[2560,1024]{1,0:T(8,128)(2,1)}, bf16[2560,256]{1,0:T(8,128)(2,1)}, bf16[2560,256]{1,0:T(8,128)(2,1)}, bf16[1024,2560]{1,0:T(8,128)(2,1)}, bf16[20,128]{1,0:T(8,128)(2,1)}) custom-call(bf16[2560,1536]{1,0:T(8,128)(2,1)S(1)} %get-tuple-element.13.rest, bf16[1024,2560]{1,0:T(8,128)(2,1)S(1)} %get-tuple-element.14.mixed, ...), custom_call_target="tpu_custom_call" | custom-call | tf_op jit(solution)/shard_map/put/pallas_call | solution.py:386

commit v4 on v3

--- a/solution.py
+++ b/solution.py
@@ -18,7 +18,12 @@
 NY, NZ = 4, 8
 SIZE = {"y": NY, "z": NZ}
 LINKS = (("y", 1), ("y", -1), ("z", 1), ("z", -1))
-RATE, LATENCY, LEAD = 46.6e3, 5.0, 6.0
+RATE, LATENCY, LEAD = 46.6e3, 6.5, 7.5
+
+
+DETOUR = {("rest", True, 0): (0, 1)}
+DETOURED = NZ // 2
+HOLD = 5.0
 
 
 def reach(n, step, side):
@@ -83,6 +88,23 @@
     return [(t, *rest) for t, _, *rest in steps]
 
 
+def with_detours(steps, pieces):
+    steps, tail = [(*s, None) for s in steps], []
+    for k, piece in enumerate(pieces):
+        step = 1 if piece["side"] == 0 else -1
+        near, far = step * (NZ // 2 - 1) % NZ, -step * (NZ // 2 - 1) % NZ
+        for dy in piece["detour"]:
+            what = [s[1:5] for s in steps]
+            usual = what.index(("send", k, (dy, far), ("z", step)))
+            ready = [w[:3] for w in what].index(("wait", k, (dy, near)))
+            steps[usual] = (*steps[usual][:5], False)
+            at = max(usual, ready)
+            steps.insert(at + 1, (steps[at][0], "send", k, (dy, near), ("z", -step), True))
+            last = [s[1:4] for s in steps].index(("wait", k, (dy, NZ // 2)))
+            tail.append(steps.pop(last))
+    return steps + tail
+
+
 def make_pieces(depth, mixed, rest):
     pieces = []
     for phase, buffer, columns in ((0, "mixed", mixed), (1, "rest", rest)):
@@ -100,6 +122,7 @@
                         col=side * columns // 2,
                         cols=columns // 2,
                         bytes=count * columns,
+                        detour=DETOUR.get((buffer, y_first, side), ()),
                     )
                 )
     return pieces
@@ -114,7 +137,7 @@
 
 def gather_kernel(n_tp, depth, *refs):
     given, (rest, mixed_out, norm_out), held = refs[:N_ARGS], refs[N_ARGS : N_ARGS + 3], refs[N_ARGS + 3 :]
-    fetched, (mixed, peers, norms, fetch_sem, sent, got, sent_norm, got_norm) = (
+    fetched, (mixed, peers, norms, fetch_sem, late, sent, sent_some, got, sent_norm, got_norm) = (
         held[:N_ARGS],
         held[N_ARGS:],
     )
@@ -141,8 +164,16 @@
     }
 
     barrier = pltpu.get_barrier_semaphore()
+    first_z, last_z = z == 0, z == NZ - 1
+
+    def greet(link, semaphore=barrier):
+        pl.semaphore_signal(semaphore, 1, device_id={"rows": to[link]}, device_id_type=MESH)
+
     for link in LINKS:
-        pl.semaphore_signal(barrier, 1, device_id={"rows": to[link]}, device_id_type=MESH)
+        if link == ("z", 1):
+            pl.when(jnp.logical_not(last_z))(functools.partial(greet, link))
+        else:
+            greet(link)
     for d in range(1, n_tp):
         pl.semaphore_signal(barrier, 1, device_id={"tp": ts[d]}, device_id_type=MESH)
 
@@ -163,12 +194,13 @@
         rest[mine, q : q + k] = merged(w_key[...], low_key[...], high_key[...])
         rest[mine, q + k :] = merged(w_value[...], low_value[...], high_value[...])
 
-    pl.semaphore_wait(barrier, len(LINKS) + n_tp - 1)
+    pl.semaphore_wait(barrier, len(LINKS) + n_tp - 1 - first_z.astype(jnp.int32))
+    pl.when(last_z)(functools.partial(greet, ("z", 1), late))
 
     buffers = {"mixed": mixed, "rest": rest}
     pieces = make_pieces(depth, mixed.shape[1], rest.shape[1])
 
-    def copy(k, origin, link):
+    def copy(k, origin, link, sent_by=None):
         p, r = pieces[k], at[origin]
         ref = buffers[p["buffer"]].at[
             pl.ds(pl.multiple_of(r * depth + p["row"], 16), p["rows"]),
@@ -177,7 +209,7 @@
         return pltpu.make_async_remote_copy(
             src_ref=ref,
             dst_ref=ref,
-            send_sem=sent.at[p["phase"]],
+            send_sem=sent.at[p["phase"]] if sent_by is None else sent_some.at[sent_by],
             recv_sem=got.at[k, r],
             device_id={"rows": to[link]},
             device_id_type=MESH,
@@ -253,7 +285,7 @@
         part = mixed[128 * j : 128 * (j + 1), :]
         mixed_out[:, 128 * j : 128 * (j + 1)] = part.T
 
-    steps = plan(pieces)
+    steps = with_detours(plan(pieces), pieces)
     turned = [s[0] for s in steps if s[1] == "wait" and pieces[s[2]]["phase"] == 0][-1]
     end = steps[-1][0]
     n_turn = mixed.shape[0] // 128
@@ -268,22 +300,47 @@
     side_jobs += [(min(s[0] for s in steps if pieces[s[2]]["phase"]) - 0.01, merge_rest)]
     side_jobs.sort(key=lambda job: job[0])
 
-    for when, what, piece, origin, link in steps:
+    first = [s[0] >= HOLD or s[1] == "wait" for s in steps].index(True)
+    down = ("z", -1)
+    held = [copy(*s[2:5]) for s in steps[:first] if s[4] == down]
+
+    def begin_down():
+        pl.semaphore_wait(late, 1)
+        for c in held:
+            c.start()
+
+    conditional = []
+    for n, (when, what, piece, origin, link, detour) in enumerate(steps):
         while side_jobs and side_jobs[0][0] < when:
             side_jobs.pop(0)[1]()
+        if n == first:
+            pl.when(first_z)(begin_down)
         if what == "wait":
             copy(piece, origin, link).wait_recv()
+        elif n < first and link == down:
+            pl.when(jnp.logical_not(first_z))(copy(piece, origin, link).start)
+        elif detour is None:
+            copy(piece, origin, link).start()
         else:
-            copy(piece, origin, link).start()
+            own = zs[origin[1]]
+            hit = own == DETOURED if detour else own != DETOURED
+            some = copy(piece, origin, link, len(conditional))
+            pl.when(hit)(some.start)
+            conditional.append((hit, some))
     for _, job in side_jobs:
         job()
 
-    n_rows = mixed.shape[0]
+    for hit, some in conditional:
+        pl.when(hit)(some.wait_send)
     for phase, buffer in ((0, mixed), (1, rest)):
-        others = buffer.at[pl.ds(0, n_rows - depth)]
+        other = buffer.shape[0] - depth
+        for p in pieces:
+            if p["phase"] == phase and p["detour"]:
+                other -= len(p["detour"]) * p["rows"] * p["cols"] // buffer.shape[1]
+        area = buffer.at[pl.ds(0, other)]
         pltpu.make_async_remote_copy(
-            src_ref=others,
-            dst_ref=others,
+            src_ref=area,
+            dst_ref=area,
             send_sem=sent.at[phase],
             recv_sem=got.at[0, 0],
             device_id={"rows": to["y", 1]},
@@ -373,7 +430,9 @@
             pltpu.VMEM((n_tp, 1, 128), f32),
             pltpu.VMEM((n_rows, 1, 128), f32),
             pltpu.SemaphoreType.DMA((N_ARGS,)),
+            pltpu.SemaphoreType.REGULAR,
             pltpu.SemaphoreType.DMA((2,)),
+            pltpu.SemaphoreType.DMA((2 * sum(len(d) for d in DETOUR.values()),)),
             pltpu.SemaphoreType.DMA((n_pieces, n_rows)),
             pltpu.SemaphoreType.DMA((13,)),
             pltpu.SemaphoreType.DMA((13,)),

time: 86.4 us -> 84.7 us (0.980)
  Pallas kernels: 85.7 us -> 83.9 us
    pallas_call x1, Pallas kernels: 80.8 us -> 79.1 us  [shards(): pl.pallas_call(functools.partial(gather_kernel, n_tp, depth), out_shape=(...]
where the time goes in v4:
time: 84.7 us; the launch traced here: 84.6 us
  Pallas kernels  83.9 us (99%)
    pallas_call x1, Pallas kernels, shards(): pl.pallas_call(functools.partial(gather_kernel, n_tp, depth), out_shape=(...  79.1 us
    pallas_call x1, Pallas kernels, shards(): pl.pallas_call(put_kernel, out_shape=(jax.ShapeDtypeStruct((total, q), bf...  4.85 us

profile of v4, /device:TPU:2, one launch (start us, length us, event | category | flops | bytes accessed | tf_op | source)
XLA Modules:
  0.0 84.6 jit_solution(8375008124752652580)
XLA Ops:
  0.6 79.1 %gather.1 = (bf16[2560,1536]{1,0:T(8,128)(2,1)S(1)}, bf16[1024,2560]{1,0:T(8,128)(2,1)S(1)}, bf16[20,128]{1,0:T(8,128)(2,1)S(1)}) custom-call(bf16[80,1024]{1,0:T(8,128)(2,1)} %refs_0_.1, bf16[64,80]{1,0:T(8,128)(2,1)} %bitcast.10, bf16[64,1024]{1,0:T(8,128)(2,1)} %refs_2_.1, bf16[80,256]{1,0:T(8,128)(2,1)} %refs_3_.1, bf16[64,80]{1,0:T(8,128)(2,1)} %bitcast.11, ...), custom_call_target="tpu_custom_call" | custom-call | tf_op jit(solution)/shard_map/gather/pallas_call | solution.py:418
  79.7 4.8 %put.1 = (bf16[2560,1024]{1,0:T(8,128)(2,1)}, bf16[2560,256]{1,0:T(8,128)(2,1)}, bf16[2560,256]{1,0:T(8,128)(2,1)}, bf16[1024,2560]{1,0:T(8,128)(2,1)}, bf16[20,128]{1,0:T(8,128)(2,1)}) custom-call(bf16[2560,1536]{1,0:T(8,128)(2,1)S(1)} %get-tuple-element.13.rest, bf16[1024,2560]{1,0:T(8,128)(2,1)S(1)} %get-tuple-element.14.mixed, ...), custom_call_target="tpu_custom_call" | custom-call | tf_op jit(solution)/shard_map/put/pallas_call | solution.py:445

commit v5 on v4

--- a/solution.py
+++ b/solution.py
@@ -23,6 +23,7 @@
 
 DETOUR = {("rest", True, 0): (0, 1)}
 DETOURED = NZ // 2
+PAIRS = True
 HOLD = 5.0
 
 
@@ -41,6 +42,25 @@
     return [(l, h) for l, h in out if h <= reach(SIZE[l[0]], l[1], piece["side"])]
 
 
+def slot_of(pieces, k, origin):
+    piece, (dy, dz) = pieces[k], origin
+    detoured = dy in piece["detour"] and dz == (NZ // 2 - 1 if piece["side"] == 0 else NZ // 2 + 1)
+    if not onward(piece, *way_of(piece, origin)) and not detoured:
+        return "last", piece["phase"]
+    if PAIRS and piece["y_first"] and dz in (1, 2, NZ - 2, NZ - 1):
+        return k - k % 2, origin
+    return k, origin
+
+
+def way_of(piece, origin):
+    dy, dz = origin
+    axis = "z" if dz and (piece["y_first"] or not dy) else "y"
+    n, off = SIZE[axis], dz if axis == "z" else dy
+    if n - off <= reach(n, 1, piece["side"]):
+        return (axis, 1), n - off
+    return (axis, -1), off
+
+
 def plan(pieces):
     def urgency(piece, link, hops):
         left = reach(SIZE[link[0]], link[1], piece["side"]) - hops
@@ -48,7 +68,11 @@
         return piece["phase"], -(left + (SIZE[second] // 2 if link[0] == first else 0))
 
     queue, free, seq = {l: [] for l in LINKS}, dict.fromkeys(LINKS, 0.0), 0
-    events, steps, got, last = [], [], {}, dict.fromkeys(LINKS, 0.0)
+    events, steps, got, ready, last = [], [], {}, {}, dict.fromkeys(LINKS, 0.0)
+    everywhere = [(k, (dy, dz)) for k in range(len(pieces)) for dy in range(NY) for dz in range(NZ) if dy or dz]
+    slots = {}
+    for k, origin in everywhere:
+        slots.setdefault(slot_of(pieces, k, origin), []).append((k, origin))
 
     def hold(k, origin, via, hops):
         nonlocal seq
@@ -57,22 +81,20 @@
             heapq.heappush(queue[link], (urgency(pieces[k], link, h), seq, k, origin, h))
 
     for k in range(len(pieces)):
-        got[k, (0, 0)] = 0.0
+        ready[k, (0, 0)] = 0.0
         hold(k, (0, 0), None, 0)
     now = 0.0
     while True:
         for link in LINKS:
             if free[link] <= now + 1e-9 and queue[link]:
                 _, _, k, origin, h = heapq.heappop(queue[link])
-                issue = max(got[k, origin], now - LEAD, last[link])
+                issue = max(ready[k, origin], now - LEAD, last[link])
                 last[link] = issue
                 seq += 1
                 steps.append((issue, seq, "send", k, origin, link))
                 free[link] = now + pieces[k]["bytes"] / RATE
-                dy, dz = origin
-                there = ((dy - link[1]) % NY, dz) if link[0] == "y" else (dy, (dz - link[1]) % NZ)
                 heapq.heappush(events, (free[link], seq, None))
-                heapq.heappush(events, (free[link] + LATENCY, seq, (k, there, link, h)))
+                heapq.heappush(events, (free[link] + LATENCY, seq, (k, beyond(origin, link), link, h)))
         if not events:
             break
         now = events[0][0]
@@ -80,29 +102,36 @@
             _, _, landed = heapq.heappop(events)
             if landed is not None:
                 k, origin, link, h = landed
-                got[k, origin] = now
-                seq += 1
-                steps.append((now, seq, "wait", k, origin, link))
-                hold(k, origin, link, h)
+                got[k, origin] = link, h
+                slot = slot_of(pieces, k, origin)
+                if all(one in got for one in slots[slot]):
+                    seq += 1
+                    steps.append((now, seq, "wait", slot, None, None))
+                    for one in slots[slot]:
+                        hold(*one, *got[one])
+                        ready[one] = now
     steps.sort(key=lambda s: (s[0], s[2] == "send", s[1]))
-    return [(t, *rest) for t, _, *rest in steps]
-
-
-def with_detours(steps, pieces):
-    steps, tail = [(*s, None) for s in steps], []
+    return [(t, *rest) for t, _, *rest in steps], slots
+
+
+def beyond(origin, link):
+    (dy, dz), (axis, step) = origin, link
+    return ((dy - step) % NY, dz) if axis == "y" else (dy, (dz - step) % NZ)
+
+
+def with_detours(steps, pieces, slots):
+    steps = [(*s, None) for s in steps]
     for k, piece in enumerate(pieces):
         step = 1 if piece["side"] == 0 else -1
         near, far = step * (NZ // 2 - 1) % NZ, -step * (NZ // 2 - 1) % NZ
         for dy in piece["detour"]:
             what = [s[1:5] for s in steps]
             usual = what.index(("send", k, (dy, far), ("z", step)))
-            ready = [w[:3] for w in what].index(("wait", k, (dy, near)))
+            slot = slot_of(pieces, k, (dy, near))
+            at = max(usual, [w[:2] for w in what].index(("wait", slot)))
             steps[usual] = (*steps[usual][:5], False)
-            at = max(usual, ready)
             steps.insert(at + 1, (steps[at][0], "send", k, (dy, near), ("z", -step), True))
-            last = [s[1:4] for s in steps].index(("wait", k, (dy, NZ // 2)))
-            tail.append(steps.pop(last))
-    return steps + tail
+    return steps
 
 
 def make_pieces(depth, mixed, rest):
@@ -200,6 +229,10 @@
     buffers = {"mixed": mixed, "rest": rest}
     pieces = make_pieces(depth, mixed.shape[1], rest.shape[1])
 
+    steps, slots = plan(pieces)
+    steps = with_detours(steps, pieces, slots)
+    numbers = {slot: n for n, slot in enumerate(slots)}
+
     def copy(k, origin, link, sent_by=None):
         p, r = pieces[k], at[origin]
         ref = buffers[p["buffer"]].at[
@@ -210,8 +243,25 @@
             src_ref=ref,
             dst_ref=ref,
             send_sem=sent.at[p["phase"]] if sent_by is None else sent_some.at[sent_by],
-            recv_sem=got.at[k, r],
+            recv_sem=got.at[numbers[slot_of(pieces, k, beyond(origin, link))]],
             device_id={"rows": to[link]},
+            device_id_type=MESH,
+        )
+
+    def arrival(slot):
+        p = pieces[slots[slot][0][0]]
+        buffer = buffers[p["buffer"]]
+        count = sum(pieces[k]["rows"] * pieces[k]["cols"] for k, _ in slots[slot])
+        if len(slots[slot]) == 1:
+            ref = buffer.at[pl.ds(0, p["rows"]), pl.ds(0, p["cols"])]
+        else:
+            ref = buffer.at[pl.ds(0, count // buffer.shape[1])]
+        return pltpu.make_async_remote_copy(
+            src_ref=ref,
+            dst_ref=ref,
+            send_sem=sent.at[0],
+            recv_sem=got.at[numbers[slot]],
+            device_id={"rows": to["y", 1]},
             device_id_type=MESH,
         )
 
@@ -285,8 +335,7 @@
         part = mixed[128 * j : 128 * (j + 1), :]
         mixed_out[:, 128 * j : 128 * (j + 1)] = part.T
 
-    steps = with_detours(plan(pieces), pieces)
-    turned = [s[0] for s in steps if s[1] == "wait" and pieces[s[2]]["phase"] == 0][-1]
+    turned = [s[0] for s in steps if s[1:3] == ("wait", ("last", 0))][0]
     end = steps[-1][0]
     n_turn = mixed.shape[0] // 128
     side_jobs = [(0.5, norm_step_0), (6.0, norm_step_1), (8.0, norm_step_2), (14.0, norm_step_3)]
@@ -297,7 +346,7 @@
     side_jobs += [
         (turned + 0.01 + gap * j, functools.partial(turn, j)) for j in range(n_turn)
     ]
-    side_jobs += [(min(s[0] for s in steps if pieces[s[2]]["phase"]) - 0.01, merge_rest)]
+    side_jobs += [(min(s[0] for s in steps if s[1] == "send" and pieces[s[2]]["phase"]) - 0.01, merge_rest)]
     side_jobs.sort(key=lambda job: job[0])
 
     first = [s[0] >= HOLD or s[1] == "wait" for s in steps].index(True)
@@ -316,7 +365,7 @@
         if n == first:
             pl.when(first_z)(begin_down)
         if what == "wait":
-            copy(piece, origin, link).wait_recv()
+            arrival(piece).wait_recv()
         elif n < first and link == down:
             pl.when(jnp.logical_not(first_z))(copy(piece, origin, link).start)
         elif detour is None:
@@ -342,7 +391,7 @@
             src_ref=area,
             dst_ref=area,
             send_sem=sent.at[phase],
-            recv_sem=got.at[0, 0],
+            recv_sem=got.at[0],
             device_id={"rows": to["y", 1]},
             device_id_type=MESH,
         ).wait_send()
@@ -397,7 +446,7 @@
     n_norm = n_rows * n_tp * norm_train.shape[0]
     bf16, f32 = jnp.bfloat16, jnp.float32
     vmem = pl.BlockSpec(memory_space=pltpu.VMEM)
-    n_pieces = len(make_pieces(depth, m, q + 2 * k))
+    n_slots = len(plan(make_pieces(depth, m, q + 2 * k))[1])
     hbm = pl.BlockSpec(memory_space=pltpu.HBM)
     given = (
         w_query,
@@ -433,7 +482,7 @@
             pltpu.SemaphoreType.REGULAR,
             pltpu.SemaphoreType.DMA((2,)),
             pltpu.SemaphoreType.DMA((2 * sum(len(d) for d in DETOUR.values()),)),
-            pltpu.SemaphoreType.DMA((n_pieces, n_rows)),
+            pltpu.SemaphoreType.DMA((n_slots,)),
             pltpu.SemaphoreType.DMA((13,)),
             pltpu.SemaphoreType.DMA((13,)),
         ],

time: 84.7 us -> 83.5 us (0.986)
  Pallas kernels: 83.9 us -> 82.7 us
    pallas_call x1, Pallas kernels: 79.1 us -> 77.9 us  [shards(): pl.pallas_call(functools.partial(gather_kernel, n_tp, depth), out_shape=(...]
where the time goes in v5:
time: 83.5 us; the launch traced here: 83.4 us
  Pallas kernels  82.7 us (99%)
    pallas_call x1, Pallas kernels, shards(): pl.pallas_call(functools.partial(gather_kernel, n_tp, depth), out_shape=(...  77.9 us
    pallas_call x1, Pallas kernels, shards(): pl.pallas_call(put_kernel, out_shape=(jax.ShapeDtypeStruct((total, q), bf...  4.85 us

profile of v5, /device:TPU:2, one launch (start us, length us, event | category | flops | bytes accessed | tf_op | source)
XLA Modules:
  0.0 83.4 jit_solution(12553871983062511608)
XLA Ops:
  0.6 77.9 %gather.1 = (bf16[2560,1536]{1,0:T(8,128)(2,1)S(1)}, bf16[1024,2560]{1,0:T(8,128)(2,1)S(1)}, bf16[20,128]{1,0:T(8,128)(2,1)S(1)}) custom-call(bf16[80,1024]{1,0:T(8,128)(2,1)} %refs_0_.1, bf16[64,80]{1,0:T(8,128)(2,1)} %bitcast.10, bf16[64,1024]{1,0:T(8,128)(2,1)} %refs_2_.1, bf16[80,256]{1,0:T(8,128)(2,1)} %refs_3_.1, bf16[64,80]{1,0:T(8,128)(2,1)} %bitcast.11, ...), custom_call_target="tpu_custom_call" | custom-call | tf_op jit(solution)/shard_map/gather/pallas_call | solution.py:467
  78.5 4.8 %put.1 = (bf16[2560,1024]{1,0:T(8,128)(2,1)}, bf16[2560,256]{1,0:T(8,128)(2,1)}, bf16[2560,256]{1,0:T(8,128)(2,1)}, bf16[1024,2560]{1,0:T(8,128)(2,1)}, bf16[20,128]{1,0:T(8,128)(2,1)}) custom-call(bf16[2560,1536]{1,0:T(8,128)(2,1)S(1)} %get-tuple-element.13.rest, bf16[1024,2560]{1,0:T(8,128)(2,1)S(1)} %get-tuple-element.14.mixed, ...), custom_call_target="tpu_custom_call" | custom-call | tf_op jit(solution)/shard_map/put/pallas_call | solution.py:494

commit v6 on v5

--- a/solution.py
+++ b/solution.py
@@ -48,7 +48,7 @@
     if not onward(piece, *way_of(piece, origin)) and not detoured:
         return "last", piece["phase"]
     if PAIRS and piece["y_first"] and dz in (1, 2, NZ - 2, NZ - 1):
-        return k - k % 2, origin
+        return k - k % 2, (dy - dy % 2, dz)
     return k, origin
 
 
@@ -405,17 +405,13 @@
 
 def put_kernel(rest, mixed, norm, final_query, final_key, final_value, final_mixed, serve_norm, sems):
     q, k = final_query.shape[1], final_key.shape[1]
-    moves = [(norm, serve_norm)]
-    for source, final, cuts in (
-        (mixed, final_mixed, 4),
-        (rest.at[:, pl.ds(0, q)], final_query, 4),
-        (rest.at[:, pl.ds(q, k)], final_key, 2),
-        (rest.at[:, pl.ds(q + k, k)], final_value, 2),
-    ):
-        count = final.shape[0] // cuts
-        for c in range(cuts):
-            part = pl.ds(c * count, count)
-            moves.append((source.at[part], final.at[part]))
+    moves = [
+        (mixed, final_mixed),
+        (rest.at[:, pl.ds(0, q)], final_query),
+        (rest.at[:, pl.ds(q, k)], final_key),
+        (rest.at[:, pl.ds(q + k, k)], final_value),
+        (norm, serve_norm),
+    ]
     copies = [pltpu.make_async_copy(a, b, sems.at[n]) for n, (a, b) in enumerate(moves)]
     for c in copies:
         c.start()
@@ -502,7 +498,7 @@
         ),
         in_specs=[vmem] * 3,
         out_specs=(hbm,) * 5,
-        scratch_shapes=[pltpu.SemaphoreType.DMA((13,))],
+        scratch_shapes=[pltpu.SemaphoreType.DMA((5,))],
         compiler_params=pltpu.CompilerParams(vmem_limit_bytes=2 << 20),
         name="put",
     )(*(pltpu.with_memory_space_constraint(a, pltpu.VMEM) for a in made))

time: 83.5 us -> 83.3 us (level)
  no operation moved by 1% of the time
where the time goes in v6:
time: 83.3 us; the launch traced here: 83.2 us
  Pallas kernels  82.5 us (99%)
    pallas_call x1, Pallas kernels, shards(): pl.pallas_call(functools.partial(gather_kernel, n_tp, depth), out_shape=(...  77.7 us
    pallas_call x1, Pallas kernels, shards(): pl.pallas_call(put_kernel, out_shape=(jax.ShapeDtypeStruct((total, q), bf...  4.8 us

profile of v6, /device:TPU:2, one launch (start us, length us, event | category | flops | bytes accessed | tf_op | source)
XLA Modules:
  0.0 83.2 jit_solution(18128894261210527751)
XLA Ops:
  0.6 77.7 %gather.1 = (bf16[2560,1536]{1,0:T(8,128)(2,1)S(1)}, bf16[1024,2560]{1,0:T(8,128)(2,1)S(1)}, bf16[20,128]{1,0:T(8,128)(2,1)S(1)}) custom-call(bf16[80,1024]{1,0:T(8,128)(2,1)} %refs_0_.1, bf16[64,80]{1,0:T(8,128)(2,1)} %bitcast.10, bf16[64,1024]{1,0:T(8,128)(2,1)} %refs_2_.1, bf16[80,256]{1,0:T(8,128)(2,1)} %refs_3_.1, bf16[64,80]{1,0:T(8,128)(2,1)} %bitcast.11, ...), custom_call_target="tpu_custom_call" | custom-call | tf_op jit(solution)/shard_map/gather/pallas_call | solution.py:463
  78.4 4.8 %put.1 = (bf16[2560,1024]{1,0:T(8,128)(2,1)}, bf16[2560,256]{1,0:T(8,128)(2,1)}, bf16[2560,256]{1,0:T(8,128)(2,1)}, bf16[1024,2560]{1,0:T(8,128)(2,1)}, bf16[20,128]{1,0:T(8,128)(2,1)}) custom-call(bf16[2560,1536]{1,0:T(8,128)(2,1)S(1)} %get-tuple-element.13.rest, bf16[1024,2560]{1,0:T(8,128)(2,1)S(1)} %get-tuple-element.14.mixed, ...), custom_call_target="tpu_custom_call" | custom-call | tf_op jit(solution)/shard_map/put/pallas_call | solution.py:490
